TPU v7x, 16 devices: a whole 2x2x2 slice. The times are simulated.
16 devices in a mesh: cp: 2 (over z), fsdp: 8 (over y, x, core).
Axes of the slice: x: 2, y: 2, z: 2, core: 2. Of those that a mesh axis runs over, the one named last changes fastest.
Arguments:
- tokens: int32 [128, 256], P('fsdp', 'cp')
- lengths: int32 [128], P('fsdp')
- embed_table: bfloat16 [33, 640], replicated
- layer_vecs: float32 [9, 640], P(None, 'fsdp')
- w_qkv: bfloat16 [640, 3, 20, 32], P('fsdp')
- w_out: bfloat16 [640, 640], P('fsdp')
- w_up: bfloat16 [640, 2560], P('fsdp')
- b_up: float32 [2560], P('fsdp')
- w_down: bfloat16 [2560, 640], P('fsdp')
- grad_out: bfloat16 [128, 256, 640], P('fsdp', 'cp')
Outputs:
- output 1: bfloat16 [128, 256, 640], P('fsdp', 'cp')
- output 2: float32 [33, 640], replicated
- output 3: float32 [9, 640], P(None, 'fsdp')
- output 4: float32 [640, 3, 20, 32], P('fsdp')
- output 5: float32 [640, 640], P('fsdp')
- output 6: float32 [640, 2560], P('fsdp')
- output 7: float32 [2560], P('fsdp')
- output 8: float32 [2560, 640], P('fsdp')
All inputs are finite; a program needn't handle non-finite values.
Results may differ from a plain program's by a relative error of at most 0.0099633.
Values are sent between devices in bfloat16 or wider.
A program may use at most 1 GiB of HBM per device.

v0:
```python
import jax
import jax.numpy as jnp
from jax import lax
from jax.sharding import PartitionSpec as P

MASK_ID = 32
LN_EPS = 1e-5
ROPE_BASE = 10000.0
TRAIN_RATIO = 0.15 * 0.8
NEG_BIG = -1e30


def layer_norm(z_in, ln_gain, ln_bias):
    row_mean = jnp.mean(z_in, axis=-1, keepdims=True)
    centered = z_in - row_mean
    row_var = jnp.mean(centered * centered, axis=-1, keepdims=True)
    return centered * lax.rsqrt(row_var + LN_EPS) * ln_gain + ln_bias


def gelu_exact(z_in):
    return jax.nn.gelu(z_in, approximate=False)


def rope_tables(positions, head_dim):
    inv_freq = 1.0 / (ROPE_BASE ** (jnp.arange(0, head_dim, 2, dtype=jnp.float32) / head_dim))
    angles = positions.astype(jnp.float32)[:, None] * inv_freq[None, :]
    return jnp.cos(angles)[:, None, :], jnp.sin(angles)[:, None, :]


def rotate(z_in, cos_t, sin_t):
    lower_half, upper_half = jnp.split(z_in, 2, axis=-1)
    return jnp.concatenate([lower_half * cos_t - upper_half * sin_t, upper_half * cos_t + lower_half * sin_t], axis=-1)


def reduce_grad(full_grad, axis_dim):
    return lax.psum(lax.psum_scatter(full_grad, 'fsdp', scatter_dimension=axis_dim, tiled=True), 'cp')


def solution(mesh):
    cp_size = mesh.shape['cp']
    send_pairs = [(dev_index, (dev_index + 1) % cp_size) for dev_index in range(cp_size)]

    def local_step(tokens, lengths, embed_table, layer_vecs, w_qkv, w_out, w_up, b_up, w_down, grad_out):
        vecs_all = lax.all_gather(layer_vecs, 'fsdp', axis=1, tiled=True)
        qkv_w = lax.all_gather(w_qkv, 'fsdp', axis=0, tiled=True)
        out_w = lax.all_gather(w_out, 'fsdp', axis=0, tiled=True)
        up_w = lax.all_gather(w_up, 'fsdp', axis=0, tiled=True)
        up_b = lax.all_gather(b_up, 'fsdp', axis=0, tiled=True)
        down_w = lax.all_gather(w_down, 'fsdp', axis=0, tiled=True)
        n_seq, seq_loc = tokens.shape
        vocab_size, model_dim = embed_table.shape
        n_heads, head_dim = qkv_w.shape[2], qkv_w.shape[3]
        cp_index = lax.axis_index('cp')
        positions = cp_index * seq_loc + jnp.arange(seq_loc)
        len_col = lengths[:, None]
        is_mask = tokens == MASK_ID
        tok_valid = positions[None, :] < len_col
        mask_count = lax.psum(jnp.sum(is_mask.astype(jnp.int32), axis=1), 'cp')
        drop_scale = (1.0 - TRAIN_RATIO) / (1.0 - mask_count.astype(jnp.float32) / lengths.astype(jnp.float32))
        keep_scale = jnp.where(is_mask | jnp.logical_not(tok_valid), 0.0, drop_scale[:, None])[:, :, None]
        one_hot = (tokens[:, :, None] == jnp.arange(vocab_size)).astype(jnp.bfloat16)
        embedded = jnp.einsum('bsv,vd->bsd', one_hot, embed_table, preferred_element_type=jnp.float32) * keep_scale
        norm_in32, ln1_pull = jax.vjp(layer_norm, embedded, vecs_all[0], vecs_all[1])
        norm_in = norm_in32.astype(jnp.bfloat16)
        qkv_lin = jnp.einsum('bsd,dthe->bsthe', norm_in, qkv_w, preferred_element_type=jnp.float32) + vecs_all[2:5].reshape(3, n_heads, head_dim)
        cos_t, sin_t = rope_tables(positions, head_dim)
        q_rot = rotate(qkv_lin[:, :, 0] * head_dim ** -0.5, cos_t, sin_t).astype(jnp.bfloat16)
        k_rot = rotate(qkv_lin[:, :, 1], cos_t, sin_t).astype(jnp.bfloat16)
        v_val = qkv_lin[:, :, 2].astype(jnp.bfloat16)

        def block_scores(k_blk, step):
            src_index = (cp_index - step) % cp_size
            key_pos = src_index * seq_loc + jnp.arange(seq_loc)
            key_ok = key_pos[None, :] < len_col
            raw_scores = jnp.einsum('bqhd,bkhd->bhqk', q_rot, k_blk, preferred_element_type=jnp.float32)
            return jnp.where(key_ok[:, None, None, :], raw_scores, NEG_BIG)

        def fwd_block(step, k_blk, v_blk, run_max, run_sum, acc_out):
            scores = block_scores(k_blk, step)
            new_max = jnp.maximum(run_max, jnp.max(scores, axis=-1))
            weights = jnp.exp(scores - new_max[..., None])
            rescale = jnp.exp(run_max - new_max)
            run_sum = run_sum * rescale + jnp.sum(weights, axis=-1)
            acc_out = acc_out * jnp.swapaxes(rescale, 1, 2)[..., None] + jnp.einsum('bhqk,bkhd->bqhd', weights.astype(jnp.bfloat16), v_blk, preferred_element_type=jnp.float32)
            return new_max, run_sum, acc_out

        def fwd_body(step, carry):
            k_blk, v_blk, run_max, run_sum, acc_out = carry
            run_max, run_sum, acc_out = fwd_block(step, k_blk, v_blk, run_max, run_sum, acc_out)
            return (lax.ppermute(k_blk, 'cp', send_pairs), lax.ppermute(v_blk, 'cp', send_pairs), run_max, run_sum, acc_out)

        stat_shape = (n_seq, n_heads, seq_loc)
        carry = (k_rot, v_val, jnp.full(stat_shape, NEG_BIG, jnp.float32), jnp.zeros(stat_shape, jnp.float32), jnp.zeros(q_rot.shape, jnp.float32))
        carry = lax.fori_loop(0, cp_size - 1, fwd_body, carry)
        run_max, run_sum, acc_out = fwd_block(cp_size - 1, carry[0], carry[1], carry[2], carry[3], carry[4])
        log_sum = run_max + jnp.log(run_sum)
        attn32 = acc_out / jnp.swapaxes(run_sum, 1, 2)[..., None]
        attn_out = attn32.astype(jnp.bfloat16).reshape(n_seq, seq_loc, model_dim)
        resid_mid = embedded + jnp.einsum('bsd,de->bse', attn_out, out_w, preferred_element_type=jnp.float32) + vecs_all[5]
        norm_mid32, ln2_pull = jax.vjp(layer_norm, resid_mid, vecs_all[6], vecs_all[7])
        norm_mid = norm_mid32.astype(jnp.bfloat16)
        up_lin = jnp.einsum('bsd,df->bsf', norm_mid, up_w, preferred_element_type=jnp.float32) + up_b
        gelu32, gelu_pull = jax.vjp(gelu_exact, up_lin)
        gelu_out = gelu32.astype(jnp.bfloat16)
        layer_out = (resid_mid + jnp.einsum('bsf,fd->bsd', gelu_out, down_w, preferred_element_type=jnp.float32) + vecs_all[8]).astype(jnp.bfloat16)

        grad32 = grad_out.astype(jnp.float32)
        d_down = jnp.einsum('bsf,bsd->fd', gelu_out, grad_out, preferred_element_type=jnp.float32)
        d_gelu = jnp.einsum('bsd,fd->bsf', grad_out, down_w, preferred_element_type=jnp.float32)
        d_up_lin = gelu_pull(d_gelu)[0]
        d_up_b = d_up_lin.astype(jnp.bfloat16)
        d_up = jnp.einsum('bsd,bsf->df', norm_mid, d_up_b, preferred_element_type=jnp.float32)
        d_norm_mid = jnp.einsum('bsf,df->bsd', d_up_b, up_w, preferred_element_type=jnp.float32)
        d_resid_ln, d_gain2, d_bias2 = ln2_pull(d_norm_mid)
        d_resid = grad32 + d_resid_ln
        d_resid_b = d_resid.astype(jnp.bfloat16)
        d_outw = jnp.einsum('bsd,bse->de', attn_out, d_resid_b, preferred_element_type=jnp.float32)
        d_attn = jnp.einsum('bse,de->bsd', d_resid_b, out_w, preferred_element_type=jnp.float32).reshape(n_seq, seq_loc, n_heads, head_dim)
        d_attn_b = d_attn.astype(jnp.bfloat16)
        delta = jnp.swapaxes(jnp.sum(d_attn * attn32, axis=-1), 1, 2)

        def bwd_block(step, k_blk, v_blk, d_query):
            scores = block_scores(k_blk, step)
            weights = jnp.exp(scores - log_sum[..., None])
            d_weights = jnp.einsum('bqhd,bkhd->bhqk', d_attn_b, v_blk, preferred_element_type=jnp.float32)
            d_scores = (weights * (d_weights - delta[..., None])).astype(jnp.bfloat16)
            d_query = d_query + jnp.einsum('bhqk,bkhd->bqhd', d_scores, k_blk, preferred_element_type=jnp.float32)
            d_key = jnp.einsum('bhqk,bqhd->bkhd', d_scores, q_rot, preferred_element_type=jnp.float32)
            d_value = jnp.einsum('bhqk,bqhd->bkhd', weights.astype(jnp.bfloat16), d_attn_b, preferred_element_type=jnp.float32)
            return d_query, d_key, d_value

        def bwd_body(step, carry):
            k_blk, v_blk, dk_blk, dv_blk, d_query = carry
            d_query, d_key, d_value = bwd_block(step, k_blk, v_blk, d_query)
            return (lax.ppermute(k_blk, 'cp', send_pairs), lax.ppermute(v_blk, 'cp', send_pairs), lax.ppermute(dk_blk + d_key, 'cp', send_pairs), lax.ppermute(dv_blk + d_value, 'cp', send_pairs), d_query)

        kv_zero = jnp.zeros(q_rot.shape, jnp.float32)
        carry = (k_rot, v_val, kv_zero, kv_zero, kv_zero)
        carry = lax.fori_loop(0, cp_size - 1, bwd_body, carry)
        d_query, d_key, d_value = bwd_block(cp_size - 1, carry[0], carry[1], carry[4])
        d_key = lax.ppermute(carry[2] + d_key, 'cp', send_pairs)
        d_value = lax.ppermute(carry[3] + d_value, 'cp', send_pairs)

        d_q_lin = rotate(d_query, cos_t, -sin_t) * head_dim ** -0.5
        d_k_lin = rotate(d_key, cos_t, -sin_t)
        d_qkv_lin = jnp.stack([d_q_lin, d_k_lin, d_value], axis=2)
        d_qkv_b = d_qkv_lin.astype(jnp.bfloat16)
        d_qkvw = jnp.einsum('bsd,bsthe->dthe', norm_in, d_qkv_b, preferred_element_type=jnp.float32)
        d_norm_in = jnp.einsum('bsthe,dthe->bsd', d_qkv_b, qkv_w, preferred_element_type=jnp.float32)
        d_embedded, d_gain1, d_bias1 = ln1_pull(d_norm_in)
        d_embedded = d_embedded + d_resid
        d_table = jnp.einsum('bsv,bsd->vd', one_hot, (d_embedded * keep_scale).astype(jnp.bfloat16), preferred_element_type=jnp.float32)
        d_bqkv = jnp.sum(d_qkv_lin, axis=(0, 1)).reshape(3, model_dim)
        d_tail = jnp.stack([jnp.sum(d_resid, axis=(0, 1)), d_gain2, d_bias2, jnp.sum(grad32, axis=(0, 1))])
        d_vecs_full = jnp.concatenate([jnp.stack([d_gain1, d_bias1]), d_bqkv, d_tail], axis=0)
        return (layer_out, lax.psum(d_table, ('cp', 'fsdp')), reduce_grad(d_vecs_full, 1), reduce_grad(d_qkvw, 0), reduce_grad(d_outw, 0), reduce_grad(d_up, 0), reduce_grad(jnp.sum(d_up_lin, axis=(0, 1)), 0), reduce_grad(d_down, 0))

    in_specs = (P('fsdp', 'cp'), P('fsdp'), P(), P(None, 'fsdp'), P('fsdp', None, None, None), P('fsdp', None), P('fsdp', None), P('fsdp'), P('fsdp', None), P('fsdp', 'cp', None))
    out_specs = (P('fsdp', 'cp', None), P(), P(None, 'fsdp'), P('fsdp', None, None, None), P('fsdp', None), P('fsdp', None), P('fsdp'), P('fsdp', None))
    return jax.shard_map(local_step, mesh=mesh, in_specs=in_specs, out_specs=out_specs, check_vma=False)
```

profile of v0, /device:TPU:0, one launch (start us, length us, event | category | flops | bytes accessed | tf_op | source)
XLA Modules:
  0.0 1263.5 jit_solution(4184291165690129981)
XLA Ops:
  12.0 11.1 all-gather
  36.0 42.2 %all-gather.5.cloned.1.call-done = bf16[640,3,20,32]{3,2,1,0:T(8,128)(2,1)} async-done(((bf16[80,3,20,32]{3,2,1,0:T(8,128)(2,1)}), bf16[640,3,20,32]{3,2,1,0:T(8,128)(2,1)}) %all-gather.5.cloned.1.call-update) | async-done | bytes 2457616 | tf_op jit(solution)/shard_map/all_gather | solution.py:45
  78.1 12.3 copy.57
  90.5 9.1 convolution_add_fusion
  111.5 23.4 %all-reduce = f32[2560]{0:T(1024)S(1)} all-reduce(f32[2560]{0:T(1024)S(1)} %dynamic-update-slice), channel_id=1, replica_groups=mesh['cp'=2,'fsdp'=8] {'fsdp'}, use_global_device_ids=true, to_apply=%add | all-reduce | flops 2560 | bytes 20480
  134.9 11.3 all_gather.20
  146.3 4.9 fusion.52
  151.6 9.6 select_reduce_fusion.1
  161.2 6.9 collective-permute-done
  168.1 10.9 select_reduce_fusion
  179.0 17.9 %fusion.6 = (f32[16,20,128]{2,1,0:T(8,128)S(1)}, f32[16,20,128]{2,1,0:T(8,128)S(1)}) fusion(f32[16,20,128,128]{2,3,1,0:T(8,128)} %get-tuple-element.136, f32[16,20,128]{2,1,0:T(8,128)S(1)} %get-tuple-element.119, pred[16,128]{1,0:T(8,128)(4,1)S(1)} %get-tuple-element.130, f32[16,20,128]{2,1,0:T(8,128)S(1)} %get-tuple-element.118, ...), kind=kLoop, calls=%fused_computation.27 | loop fusion | flops 31375360 | bytes 42602496 | tf_op jit(solution)/shard_map/while/body/eval_jaxpr/reduce_sum | solution.py:83
  197.8 14.4 %fusion.20 = f32[16,20,32,128]{3,2,1,0:T(8,128)} fusion(f32[16,20,128,128]{2,3,1,0:T(8,128)} %get-tuple-element.136, f32[16,20,128]{2,1,0:T(8,128)S(1)} %get-tuple-element.119, pred[16,128]{1,0:T(8,128)(4,1)S(1)} %get-tuple-element.130, f32[16,128,3,20,32]{1,4,3,2,0:T(8,128)} %copy-done.5), kind=kOutput, calls=%fused_computation.41 | convolution fusion | flops 351272960 | bytes 29001728 | tf_op jit(solution)/shard_map/while/body/eval_jaxpr/bhqk,bkhd->bqhd/dot_general | solution.py:84
  212.2 11.3 collective-permute-done.1
  223.6 14.4 %fusion.99 = (bf16[16,128,20,32]{1,3,2,0:T(8,128)(2,1)S(1)}, f32[16,128,20,32]{1,3,2,0:T(8,128)}) fusion(f32[16,128,20]{1,2,0:T(8,128)} %get-tuple-element.116, bf16[16,128,20,32]{1,3,2,0:T(8,128)(2,1)} %collective-permute-done.1, f32[16,20,128,128]{2,3,1,0:T(8,128)} %get-tuple-element.134, f32[16,20,128]{2,1,0:T(8,128)} %copy-done.24, ...), kind=kOutput, calls=%fused_computation.187 | convolution fusion | flops 357826560 | bytes 37357568 | tf_op jit(solution)/shard_map/bhqk,bkhd->bqhd/dot_general | solution.py:84
  244.6 19.9 %fusion.31 = (u16[128,2560]{1,0:T(8,128)(2,1)S(1)}, u16[128,2560]{1,0:T(8,128)(2,1)S(1)}, f32[16,128,2560]{2,1,0:T(8,128)}) fusion(f32[2560]{0:T(1024)S(1)} %all-reduce, bf16[640,2560]{1,0:T(8,128)(2,1)} %all-gather.7.cloned.1.call-done, f32[16,128,640]{2,1,0:T(8,128)} %copy-done.3, f32[640]{0:T(1024)S(1)} %get-tuple-element.77, ...), kind=kOutput, calls=%fused_computation.51 | convolution fusion | flops 6790184960 | bytes 30833664 | tf_op jit(solution)/shard_map/bsd,df->bsf/dot_general | solution.py:102
  264.5 50.5 %multiply_convert_fusion.2 = (bf16[16,128,2560]{2,1,0:T(8,128)(2,1)}, f32[16,128,2560]{2,1,0:T(8,128)}) fusion(f32[16,128,2560]{2,1,0:T(8,128)} %get-tuple-element.141, f32[2560]{0:T(1024)S(1)} %all-reduce, u16[128,2560]{1,0:T(8,128)(2,1)S(1)} %get-tuple-element.52, u16[128,2560]{1,0:T(8,128)(2,1)S(1)} %get-tuple-element.51), kind=kLoop, calls=%fused_computation.12 | loop fusion | flops 372244480 | bytes 53749760 | tf_op jit(solution)/shard_map/convert_element_type | solution.py:104
  315.2 26.4 %fusion.101 = (f32[2560]{0:T(1024)}, bf16[16,128,2560]{2,1,0:T(8,128)(2,1)}) fusion(f32[16,128,2560]{2,1,0:T(8,128)} %get-tuple-element.103, bf16[16,128,640]{2,1,0:T(8,128)(2,1)} %param.19, bf16[2560,640]{1,0:T(8,128)(2,1)} %all-gather.9.cloned.1.call-done, f32[16,128,2560]{2,1,0:T(8,128)} %get-tuple-element.141, f32[2560]{0:T(1024)S(1)} %all-reduce), kind=kOutput, calls=%fused_computation.189 | convolution fusion | flops 6794769920 | bytes 58347520 | tf_op jit(solution)/shard_map/bsd,fd->bsf/dot_general | solution.py:109
  341.6 11.7 multiply_reduce_fusion
  362.8 15.7 %multiply_convert_fusion.1 = bf16[16,20,128,128]{2,3,1,0:T(8,128)(2,1)} fusion(f32[16,20,128,128]{2,3,1,0:T(8,128)} %get-tuple-element.136, f32[16,20,128]{2,1,0:T(8,128)S(1)} %bitcast.194, f32[16,20,128]{2,1,0:T(8,128)S(1)} %log_add_fusion, pred[16,128]{1,0:T(8,128)(4,1)S(1)} %get-tuple-element.130, bf16[16,128,20,32]{1,3,2,0:T(8,128)(2,1)S(1)} %convert_element_type.92, ...), kind=kOutput, calls=%fused_computation.9 | convolution fusion | flops 361758720 | bytes 37029888 | tf_op jit(solution)/shard_map/while/body/eval_jaxpr/bqhd,bkhd->bhqk/dot_general | solution.py:125
  378.6 12.7 %convolution_bitcast_fusion.2 = f32[16,128,20,32]{1,3,2,0:T(8,128)} fusion(bf16[16,20,128,128]{2,3,1,0:T(8,128)(2,1)} %multiply_convert_fusion.1, bf16[16,128,20,16]{1,3,2,0:T(8,128)(2,1)} %copy-done.6, bf16[16,128,20,16]{1,3,2,0:T(8,128)(2,1)} %copy-done.7), kind=kOutput, calls=%fused_computation.122 | convolution fusion | flops 340787200 | bytes 18350080 | tf_op jit(solution)/shard_map/while/body/eval_jaxpr/bhqk,bqhd->bkhd/dot_general | solution.py:128
  392.7 11.6 fusion.60
  404.8 15.4 %multiply_convert_fusion = bf16[16,20,128,128]{2,3,1,0:T(8,128)(2,1)} fusion(f32[16,20,128,128]{2,3,1,0:T(8,128)} %get-tuple-element.134, f32[16,20,128]{2,1,0:T(8,128)S(1)} %bitcast.195, f32[16,20,128]{2,1,0:T(8,128)S(1)} %log_add_fusion, pred[16,128]{1,0:T(8,128)(4,1)S(1)} %copy-done.39, bf16[16,128,20,32]{1,3,2,0:T(8,128)(2,1)S(1)} %convert_element_type.92, ...), kind=kOutput, calls=%fused_computation.7 | convolution fusion | flops 361758720 | bytes 37029888 | tf_op jit(solution)/shard_map/bqhd,bkhd->bhqk/dot_general | solution.py:125
  420.3 86.9 %collective-permute-done.2 = f32[16,128,20,32]{1,3,2,0:T(8,128)} collective-permute-done((f32[16,128,20,32]{1,3,2,0:T(8,128)}, f32[16,128,20,32]{1,3,2,0:T(8,128)}, u32[]{:S(2)}, u32[]{:S(2)}) %collective-permute-start.2) | collective-permute-done | bytes 5242912 | tf_op jit(solution)/shard_map/while/body/eval_jaxpr/ppermute | solution.py:135
  507.1 14.1 %bitcast_add_fusion.1 = f32[16,128,20,32]{1,3,2,0:T(8,128)} fusion(f32[16,128,20,32]{1,3,2,0:T(8,128)} %collective-permute-done.2, bf16[16,20,128,128]{2,3,1,0:T(8,128)(2,1)} %multiply_convert_fusion, bf16[16,128,20,16]{1,3,2,0:T(8,128)(2,1)} %copy-done.6, bf16[16,128,20,16]{1,3,2,0:T(8,128)(2,1)} %copy-done.7), kind=kOutput, calls=%fused_computation.77 | convolution fusion | flops 342097920 | bytes 23592960 | tf_op jit(solution)/shard_map/bhqk,bqhd->bkhd/dot_general | solution.py:128
  522.7 96.8 %collective-permute-done.4 = f32[16,128,20,32]{1,3,2,0:T(8,128)} collective-permute-done((f32[16,128,20,32]{1,3,2,0:T(8,128)}, f32[16,128,20,32]{1,3,2,0:T(8,128)}, u32[]{:S(2)}, u32[]{:S(2)}) %collective-permute-start.4) | collective-permute-done | bytes 5242912 | tf_op jit(solution)/shard_map/while/body/eval_jaxpr/ppermute | solution.py:135
  619.5 12.9 %bitcast_add_fusion = f32[16,128,20,32]{1,3,2,0:T(8,128)} fusion(f32[16,128,20,32]{1,3,2,0:T(8,128)} %collective-permute-done.4, bf16[16,128,20,32]{1,3,2,0:T(8,128)(2,1)S(1)} %convert_element_type.92, f32[16,20,128,128]{2,3,1,0:T(8,128)} %get-tuple-element.134, f32[16,20,128]{2,1,0:T(8,128)S(1)} %log_add_fusion, pred[16,128]{1,0:T(8,128)(4,1)S(1)} %copy-done.39), kind=kOutput, calls=%fused_computation.76 | convolution fusion | flops 352583680 | bytes 34244608 | tf_op jit(solution)/shard_map/bhqk,bqhd->bkhd/dot_general | solution.py:129
  633.9 6.3 fusion.95
  640.1 6.6 add_bitcast_fusion
  646.7 85.1 %collective-permute-done.3 = f32[16,128,20,32]{1,3,2,0:T(8,128)} collective-permute-done((f32[16,128,20,32]{1,3,2,0:T(8,128)}, f32[16,128,20,32]{1,3,2,0:T(8,128)}, u32[]{:S(2)}, u32[]{:S(2)}) %collective-permute-start.3) | collective-permute-done | bytes 5242912 | tf_op jit(solution)/shard_map/ppermute | solution.py:141
  731.8 6.7 subtract_bitcast_fusion
  738.5 5.8 maximum_multiply_fusion
  747.3 95.4 %collective-permute-done.5 = f32[16,128,20,32]{1,3,2,0:T(8,128)} collective-permute-done((f32[16,128,20,32]{1,3,2,0:T(8,128)}, f32[16,128,20,32]{1,3,2,0:T(8,128)}, u32[]{:S(2)}, u32[]{:S(2)}) %collective-permute-start.5) | collective-permute-done | bytes 5242912 | tf_op jit(solution)/shard_map/ppermute | solution.py:142
  842.8 14.5 %fusion.53 = f32[640,3,20,32,1]{0,3,2,4,1:T(8,128)} fusion(f32[16,128,640]{2,1,0:T(8,128)S(1)} %bitcast.180, f32[640]{0:T(1024)S(1)} %copy-done.48, f32[640]{0:T(1024)S(1)} %copy-done.41, f32[16,128]{1,0:T(8,128)S(1)} %copy-done.33, f32[16,128]{1,0:T(8,128)S(1)} %copy-done.28, f32[16,128]{1,0:T(8,128)S(1)} %copy-done.26, ...), kind=kOutput, calls=%fused_computation.106 | convolution fusion | flops 5064622080 | bytes 25916416 | tf_op jit(solution)/shard_map/bsd,bsthe->dthe/dot_general | solution.py:148
  857.3 5.9 copy.100
  863.3 6.0 convolution_bitcast_fusion.3
  869.4 13.3 %convolution_bitcast_fusion = f32[2560,640]{1,0:T(8,128)} fusion(bf16[16,128,2560]{2,1,0:T(8,128)(2,1)} %get-tuple-element.102, bf16[16,128,640]{2,1,0:T(8,128)(2,1)S(1)} %copy-done.13), kind=kOutput, calls=%fused_computation.63 | convolution fusion | flops 6710886400 | bytes 19660800 | tf_op jit(solution)/shard_map/bsf,bsd->fd/dot_general | solution.py:108
  883.4 13.6 %convolution_bitcast_fusion.1 = f32[640,2560]{1,0:T(8,128)} fusion(bf16[16,128,2560]{2,1,0:T(8,128)(2,1)} %get-tuple-element.145, f32[16,128,640]{2,1,0:T(8,128)} %copy-done.3, f32[640]{0:T(1024)S(1)} %copy-done.46, f32[640]{0:T(1024)S(1)} %get-tuple-element.75, f32[16,128]{1,0:T(8,128)S(1)} %fusion.83, f32[16,128]{1,0:T(8,128)S(1)} %broadcast_multiply_fusion), kind=kOutput, calls=%fused_computation.64 | convolution fusion | flops 6717440000 | bytes 22303744 | tf_op jit(solution)/shard_map/bsd,bsf->df/dot_general | solution.py:112
  897.1 34.4 %bitcast_reduce_fusion = (f32[640]{0:T(1024)S(1)}, f32[16,128]{1,0:T(8,128)S(1)}, f32[16,128,640,1,1]{2,1,3,0,4:T(8,128)}) fusion(f32[640]{0:T(1024)S(1)} %copy-done.41, f32[16,128]{1,0:T(8,128)S(1)} %copy-done.28, f32[16,128,640]{2,1,0:T(8,128)} %copy-done.2, f32[16,128]{1,0:T(8,128)S(1)} %copy-done.26, bf16[640,3,20,32,1]{3,2,1,0,4:T(8,128)(2,1)} %bitcast.187, ...), kind=kOutput, calls=%fused_computation.72 | convolution fusion | flops 5048890880 | bytes 28701696 | tf_op jit(solution)/shard_map/bsthe,dthe->bsd/dot_general | solution.py:149
  931.5 4.5 fusion.40
  936.1 6.7 fusion.12
  943.9 7.9 fusion.69
  954.3 54.3 %reduce-scatter.14.cloned.1.call-done = f32[320,640]{1,0:T(8,128)} async-done(((f32[2560,640]{1,0:T(8,128)}), f32[320,640]{1,0:T(8,128)}) %reduce-scatter.14.cloned.1.call-update) | async-done | bytes 819216 | tf_op jit(solution)/shard_map/reduce_scatter | solution.py:36
  1008.7 60.2 %reduce-scatter.12.cloned.1.call-done = f32[80,2560]{1,0:T(8,128)} async-done(((f32[640,2560]{1,0:T(8,128)}), f32[80,2560]{1,0:T(8,128)}) %reduce-scatter.12.cloned.1.call-update) | async-done | bytes 819216 | tf_op jit(solution)/shard_map/reduce_scatter | solution.py:36
  1069.4 23.2 %all-reduce.1 = f32[2560]{0:T(1024)S(1)} all-reduce(f32[2560]{0:T(1024)S(1)} %copy-done.43), channel_id=6, replica_groups=mesh['cp'=2,'fsdp'=8] {'fsdp'}, use_global_device_ids=true, to_apply=%region_32.33.clone | all-reduce | flops 2560 | bytes 20480
  1092.7 13.8 %add_convert_fusion = bf16[16,128,640]{2,1,0:T(8,128)(2,1)} fusion(f32[16,128,640]{2,1,0:T(8,128)} %copy-done.3, f32[640]{0:T(1024)S(1)} %copy-done.44, bf16[16,128,2560]{2,1,0:T(8,128)(2,1)} %get-tuple-element.102, bf16[2560,640]{1,0:T(8,128)(2,1)} %all-gather.9.cloned.1.call-done), kind=kOutput, calls=%fused_computation.91 | convolution fusion | flops 6714818560 | bytes 21629440 | tf_op jit(solution)/shard_map/bsf,fd->bsd/dot_general | solution.py:105
  1107.4 8.6 all-reduce.2
  1116.0 54.6 %all-reduce.7.cloned.1.call-done = f32[33,640]{1,0:T(8,128)} async-done(((f32[33,640]{1,0:T(8,128)}), f32[33,640]{1,0:T(8,128)}) %all-reduce.7.cloned.1.call-update) | async-done | bytes 84496 | tf_op jit(solution)/shard_map/psum | solution.py:156
  1170.5 76.3 %all-reduce.9.cloned.1.call-done = (f32[80,3,20,32]{0,3,2,1:T(8,128)}, f32[80,640]{1,0:T(8,128)}, f32[80,2560]{1,0:T(8,128)}, f32[320,640]{1,0:T(8,128)}) async-done(((f32[80,3,20,32]{0,3,2,1:T(8,128)}, f32[80,640]{1,0:T(8,128)}, f32[80,2560]{1,0:T(8,128)}, f32[320,640]{1,0:T(8,128)}), (f32[80,3,20,32]{0,3,2,1:T(8,128)}, f32[80,640]{1,0:T(8,128)}, f32[80,2560]{1,0:T(8,128)}, ...) | async-done | bytes 2457616 | tf_op jit(solution)/shard_map/psum | solution.py:36
  (224 shorter events, 69.2 us)
Async XLA Ops:
  7.2 70.9 %all-gather.5.cloned.1.call-start = ((), (), s32[]{:S(2)}) async-start(), calls=%async_computation.5 | async-start | bytes 13271040 | tf_op jit(solution)/shard_map/all_gather | solution.py:45
  10.4 234.2 %all-gather.7.cloned.1.call-start = ((), (), s32[]{:S(2)}) async-start(), calls=%async_computation.6 | async-start | bytes 3686400 | tf_op jit(solution)/shard_map/all_gather | solution.py:47
  11.1 304.0 %all-gather.9.cloned.1.call-start = ((), (), s32[]{:S(2)}) async-start(), calls=%async_computation.7 | async-start | bytes 3686400 | tf_op jit(solution)/shard_map/all_gather | solution.py:49
  23.8 66.6 %copy-start.40 = (f32[640]{0:T(1024)}, f32[640]{0:T(1024)S(1)}, u32[]{:S(2)}) copy-start(f32[640]{0:T(1024)S(1)} %get-tuple-element.93) | copy-start | bytes 7684
  23.8 66.6 %copy-start.47 = (f32[640]{0:T(1024)}, f32[640]{0:T(1024)S(1)}, u32[]{:S(2)}) copy-start(f32[640]{0:T(1024)S(1)} %get-tuple-element.92) | copy-start | bytes 7684
  23.8 220.8 %copy-start.45 = (f32[640]{0:T(1024)}, f32[640]{0:T(1024)S(1)}, u32[]{:S(2)}) copy-start(f32[640]{0:T(1024)S(1)} %get-tuple-element.77) | copy-start | bytes 7684
  29.6 208.4 %copy-start.25 = (f32[16,128]{1,0:T(8,128)}, f32[16,128]{1,0:T(8,128)S(1)}, u32[]{:S(2)}) copy-start(f32[16,128]{1,0:T(8,128)S(1)} %or_select_fusion) | copy-start | bytes 24580
  31.4 59.1 %copy-start.27 = (f32[16,128]{1,0:T(8,128)}, f32[16,128]{1,0:T(8,128)S(1)}, u32[]{:S(2)}) copy-start(f32[16,128]{1,0:T(8,128)S(1)} %broadcast_multiply_fusion.1) | copy-start | bytes 24580
  35.3 55.2 %copy-start.32 = (f32[16,128]{1,0:T(8,128)}, f32[16,128]{1,0:T(8,128)S(1)}, u32[]{:S(2)}) copy-start(f32[16,128]{1,0:T(8,128)S(1)} %fusion.82) | copy-start | bytes 24580
  36.0 65.1 %copy-start.29 = (f32[128,16]{0,1:T(8,128)}, f32[128,16]{0,1:T(8,128)S(1)}, u32[]{:S(2)}) copy-start(f32[128,16]{0,1:T(8,128)S(1)} %get-tuple-element.126) | copy-start | bytes 24580
  105.1 63.0 %copy-start.6 = (bf16[16,128,20,16]{1,3,2,0:T(8,128)(2,1)}, bf16[16,128,20,16]{1,3,2,0:T(8,128)(2,1)S(1)}, u32[]{:S(2)}) copy-start(bf16[16,128,20,16]{1,3,2,0:T(8,128)(2,1)S(1)} %get-tuple-element.122) | copy-start | bytes 3932164
  105.1 63.0 %copy-start.7 = (bf16[16,128,20,16]{1,3,2,0:T(8,128)(2,1)}, bf16[16,128,20,16]{1,3,2,0:T(8,128)(2,1)S(1)}, u32[]{:S(2)}) copy-start(bf16[16,128,20,16]{1,3,2,0:T(8,128)(2,1)S(1)} %get-tuple-element.123) | copy-start | bytes 3932164
  105.2 41.1 %copy-start.51 = (s32[16]{0:T(128)S(1)}, s32[16]{0:T(128)}, u32[]{:S(2)}) copy-start(s32[16]{0:T(128)} %param.11) | copy-start | bytes 196
  108.3 59.7 %collective-permute-start = (bf16[16,128,20,32]{1,3,2,0:T(8,128)(2,1)}, bf16[16,128,20,32]{1,3,2,0:T(8,128)(2,1)}, u32[]{:S(2)}, u32[]{:S(2)}) collective-permute-start(bf16[16,128,20,32]{1,3,2,0:T(8,128)(2,1)} %pad_maximum_fusion.2), channel_id=1, source_target_pairs={{0,8},{8,0},{1,9},{9,1},{2,10},{10,2},{3,11},{11,3},{4,12},{12,4},... | collective-permute-start | bytes 7864328 | tf_op jit(solution)/shard_map/while/body/eval_jaxpr/ppermute | solution.py:90
  109.8 842.1 %reduce-scatter.18.cloned.1.call-start = ((), (), s32[]{:S(2)}) async-start(), calls=%async_computation.13 | async-start | bytes 5529600
  146.2 91.7 %copy-start.16 = (bf16[640,640]{1,0:T(8,128)(2,1)}, bf16[640,640]{1,0:T(8,128)(2,1)S(1)}, u32[]{:S(2)}) copy-start(bf16[640,640]{1,0:T(8,128)(2,1)S(1)} %all_gather.20) | copy-start | bytes 2457604
  146.3 77.2 %copy-start.38 = (pred[16,128]{1,0:T(8,128)(4,1)}, pred[16,128]{1,0:T(8,128)(4,1)S(1)}, u32[]{:S(2)}) copy-start(pred[16,128]{1,0:T(8,128)(4,1)S(1)} %get-tuple-element.129) | copy-start | bytes 6148
  151.2 72.4 %collective-permute-start.1 = (bf16[16,128,20,32]{1,3,2,0:T(8,128)(2,1)}, bf16[16,128,20,32]{1,3,2,0:T(8,128)(2,1)}, u32[]{:S(2)}, u32[]{:S(2)}) collective-permute-start(bf16[16,128,20,32]{1,3,2,0:T(8,128)(2,1)} %fusion.52), channel_id=1, source_target_pairs={{0,8},{8,0},{1,9},{9,1},{2,10},{10,2},{3,11},{11,3},{4,12},{12,4},... | collective-permute-start | bytes 7864328 | tf_op jit(solution)/shard_map/while/body/eval_jaxpr/ppermute | solution.py:90
  161.2 35.8 %copy-start.18 = (f32[16,20,128]{2,1,0:T(8,128)}, f32[16,20,128]{2,1,0:T(8,128)S(1)}, u32[]{:S(2)}) copy-start(f32[16,20,128]{2,1,0:T(8,128)S(1)} %get-tuple-element.135) | copy-start | bytes 491524
  197.8 40.1 %slice-start = ((s8[5242880]{0:T(1024)(128)(4,1)}), s8[1048576]{0:T(1024)(128)(4,1)S(1)}, s32[]{:S(2)}) async-start(s8[5242880]{0:T(1024)(128)(4,1)} %bitcast.177), calls=%async_computation.15 | async-start | bytes 2097152
  264.5 50.5 %copy-start.19 = (f32[16,20,128]{2,1,0:T(8,128)S(1)}, f32[16,20,128]{2,1,0:T(8,128)}, u32[]{:S(2)}) copy-start(f32[16,20,128]{2,1,0:T(8,128)} %copy-done.18) | copy-start | bytes 491524
  264.5 50.5 %copy-start.21 = (f32[16,20,128]{2,1,0:T(8,128)S(1)}, f32[16,20,128]{2,1,0:T(8,128)}, u32[]{:S(2)}) copy-start(f32[16,20,128]{2,1,0:T(8,128)} %copy-done.20) | copy-start | bytes 491524
  264.5 77.1 %slice-start.6 = ((s8[5242880]{0:T(1024)(128)(4,1)}), s8[1048576]{0:T(1024)(128)(4,1)S(1)}, s32[]{:S(2)}) async-start(s8[5242880]{0:T(1024)(128)(4,1)} %bitcast.183), calls=%async_computation.21 | async-start | bytes 2097152
  391.2 115.9 %collective-permute-start.2 = (f32[16,128,20,32]{1,3,2,0:T(8,128)}, f32[16,128,20,32]{1,3,2,0:T(8,128)}, u32[]{:S(2)}, u32[]{:S(2)}) collective-permute-start(f32[16,128,20,32]{1,3,2,0:T(8,128)} %convolution_bitcast_fusion.2), channel_id=1, source_target_pairs={{0,8},{8,0},{1,9},{9,1},{2,10},{10,2},{3,11},{11,3},{4,12},{12,4},... | collective-permute-start | bytes 15728648 | tf_op jit(solution)/shard_map/while/body/eval_jaxpr/ppermute | solution.py:135
  404.3 215.2 %collective-permute-start.4 = (f32[16,128,20,32]{1,3,2,0:T(8,128)}, f32[16,128,20,32]{1,3,2,0:T(8,128)}, u32[]{:S(2)}, u32[]{:S(2)}) collective-permute-start(f32[16,128,20,32]{1,3,2,0:T(8,128)} %fusion.60), channel_id=1, source_target_pairs={{0,8},{8,0},{1,9},{9,1},{2,10},{10,2},{3,11},{11,3},{4,12},{12,4},... | collective-permute-start | bytes 15728648 | tf_op jit(solution)/shard_map/while/body/eval_jaxpr/ppermute | solution.py:135
  521.3 210.6 %collective-permute-start.3 = (f32[16,128,20,32]{1,3,2,0:T(8,128)}, f32[16,128,20,32]{1,3,2,0:T(8,128)}, u32[]{:S(2)}, u32[]{:S(2)}) collective-permute-start(f32[16,128,20,32]{1,3,2,0:T(8,128)} %bitcast_add_fusion.1), channel_id=1, source_target_pairs={{0,8},{8,0},{1,9},{9,1},{2,10},{10,2},{3,11},{11,3},{4,12},{12,4},... | collective-permute-start | bytes 15728648 | tf_op jit(solution)/shard_map/ppermute | solution.py:141
  632.4 210.3 %collective-permute-start.5 = (f32[16,128,20,32]{1,3,2,0:T(8,128)}, f32[16,128,20,32]{1,3,2,0:T(8,128)}, u32[]{:S(2)}, u32[]{:S(2)}) collective-permute-start(f32[16,128,20,32]{1,3,2,0:T(8,128)} %bitcast_add_fusion), channel_id=1, source_target_pairs={{0,8},{8,0},{1,9},{9,1},{2,10},{10,2},{3,11},{11,3},{4,12},{12,4},... | collective-permute-start | bytes 15728648 | tf_op jit(solution)/shard_map/ppermute | solution.py:142
  640.1 91.7 %copy-start.30 = (f32[128,16]{0,1:T(8,128)S(1)}, f32[128,16]{0,1:T(8,128)}, u32[]{:S(2)}) copy-start(f32[128,16]{0,1:T(8,128)} %copy-done.29) | copy-start | bytes 24580
  640.1 91.7 %copy-start.42 = (f32[128,16]{0,1:T(8,128)S(1)}, f32[128,16]{0,1:T(8,128)}, u32[]{:S(2)}) copy-start(f32[128,16]{0,1:T(8,128)} %get-tuple-element.124) | copy-start | bytes 24580
  738.5 104.2 %slice-start.2 = ((s8[5242880]{0:T(1024)(128)(4,1)}), s8[4194304]{0:T(1024)(128)(4,1)S(1)}, s32[]{:S(2)}) async-start(s8[5242880]{0:T(1024)(128)(4,1)} %bitcast.179), calls=%async_computation.17 | async-start | bytes 8388608
  744.3 98.4 %slice-start.3 = ((s8[5242880]{0:T(1024)(128)(4,1)}), s8[1048576]{0:T(1024)(128)(4,1)S(1)}, s32[]{:S(2)}) async-start(s8[5242880]{0:T(1024)(128)(4,1)} %bitcast.179), calls=%async_computation.18 | async-start | bytes 2097152
  744.3 98.4 %copy-start.26 = (f32[16,128]{1,0:T(8,128)S(1)}, f32[16,128]{1,0:T(8,128)}, u32[]{:S(2)}) copy-start(f32[16,128]{1,0:T(8,128)} %copy-done.25) | copy-start | bytes 24580
  744.3 98.4 %copy-start.28 = (f32[16,128]{1,0:T(8,128)S(1)}, f32[16,128]{1,0:T(8,128)}, u32[]{:S(2)}) copy-start(f32[16,128]{1,0:T(8,128)} %copy-done.27) | copy-start | bytes 24580
  744.3 98.4 %copy-start.33 = (f32[16,128]{1,0:T(8,128)S(1)}, f32[16,128]{1,0:T(8,128)}, u32[]{:S(2)}) copy-start(f32[16,128]{1,0:T(8,128)} %copy-done.32) | copy-start | bytes 24580
  744.4 98.4 %copy-start.41 = (f32[640]{0:T(1024)S(1)}, f32[640]{0:T(1024)}, u32[]{:S(2)}) copy-start(f32[640]{0:T(1024)} %copy-done.40) | copy-start | bytes 7684
  744.4 98.4 %copy-start.48 = (f32[640]{0:T(1024)S(1)}, f32[640]{0:T(1024)}, u32[]{:S(2)}) copy-start(f32[640]{0:T(1024)} %copy-done.47) | copy-start | bytes 7684
  863.2 91.1 %reduce-scatter.10.cloned.1.call-start = ((), (), s32[]{:S(2)}) async-start(), calls=%async_computation.9 | async-start | bytes 1843200 | tf_op jit(solution)/shard_map/reduce_scatter | solution.py:36
  869.3 139.4 %reduce-scatter.14.cloned.1.call-start = ((), (), s32[]{:S(2)}) async-start(), calls=%async_computation.11 | async-start | bytes 7372800 | tf_op jit(solution)/shard_map/reduce_scatter | solution.py:36
  882.7 186.1 %reduce-scatter.12.cloned.1.call-start = ((), (), s32[]{:S(2)}) async-start(), calls=%async_computation.10 | async-start | bytes 7372800 | tf_op jit(solution)/shard_map/reduce_scatter | solution.py:36
  896.9 34.6 %slice-start.4 = ((s8[5242880]{0:T(1024)(128)(4,1)}), s8[1048576]{0:T(1024)(128)(4,1)S(1)}, s32[]{:S(2)}) async-start(s8[5242880]{0:T(1024)(128)(4,1)} %bitcast.181), calls=%async_computation.19 | async-start | bytes 2097152
  897.0 209.5 %reduce-scatter.16.cloned.1.call-start = ((), (), s32[]{:S(2)}) async-start(), calls=%async_computation.12 | async-start | bytes 368640
  897.1 34.4 %copy-start.37 = (f32[16,128]{1,0:T(8,128)S(1)}, f32[16,128]{1,0:T(8,128)}, u32[]{:S(2)}) copy-start(f32[16,128]{1,0:T(8,128)} %copy-done.36) | copy-start | bytes 24580
  897.1 34.4 %slice-start.5 = ((s8[5242880]{0:T(1024)(128)(4,1)}), s8[4194304]{0:T(1024)(128)(4,1)S(1)}, s32[]{:S(2)}) async-start(s8[5242880]{0:T(1024)(128)(4,1)} %bitcast.181), calls=%async_computation.20 | async-start | bytes 8388608
  943.8 125.6 %copy-start.43 = (f32[2560]{0:T(1024)S(1)}, f32[2560]{0:T(1024)}, u32[]{:S(2)}) copy-start(f32[2560]{0:T(1024)} %get-tuple-element.144) | copy-start | bytes 30724
  943.8 148.8 %copy-start.44 = (f32[640]{0:T(1024)S(1)}, f32[640]{0:T(1024)}, u32[]{:S(2)}) copy-start(f32[640]{0:T(1024)} %get-tuple-element.76) | copy-start | bytes 7684
  943.9 226.7 %all-reduce.7.cloned.1.call-start = ((), (), s32[]{:S(2)}) async-start(), calls=%async_computation.8 | async-start | bytes 204800 | tf_op jit(solution)/shard_map/psum | solution.py:156
  951.9 295.0 %all-reduce.9.cloned.1.call-start = ((), (), s32[]{:S(2)}) async-start(), calls=%async_computation.14 | async-start | bytes 5652480 | tf_op jit(solution)/shard_map/psum | solution.py:36
  1092.7 163.7 %copy-start.1 = (bf16[33,640]{1,0:T(8,128)(2,1)S(1)}, bf16[33,640]{1,0:T(8,128)(2,1)}, u32[]{:S(2)}) copy-start(bf16[33,640]{1,0:T(8,128)(2,1)} %param.12) | copy-start | bytes 126724
  (31 other events, 259.0 us)
Sparse Core Ops, SparseCore 0:
  10.5 67.5 all-gather.4
  80.0 28.7 all-gather.6
  110.6 28.8 all-gather.8
  863.3 48.6 reduce-scatter.17
  915.8 32.8 reduce-scatter.9
  951.9 56.7 reduce-scatter.13
  1012.1 56.6 reduce-scatter.11
  1072.4 28.1 reduce-scatter.15
  1105.4 65.0 all-reduce.6
  1173.5 73.3 all-reduce.8
where the time goes:
time: 1270 us; the launch traced here: 1260 us
  waiting for transfers between devices  671 us (53%)
  matrix products  323 us (25%)
  other arithmetic  111 us (9%)
  blocking collectives  81.8 us (6%)
  local copies, waits for them, and re-layouts  53 us (4%)
  between operations  16.6 us (1%)
    reduce_scatter x3, waiting for transfers between devices, reduce_grad(): lax.psum_scatter(full_grad, 'fsdp', scatter_dimension=axis_dim, tiled=True)  114 us
    ppermute x1, waiting for transfers between devices, bwd_body(): lax.ppermute(dv_blk + d_value, 'cp', send_pairs)  96.8 us
    ppermute x1, waiting for transfers between devices, local_step(): d_value = lax.ppermute(carry[3] + d_value, 'cp', send_pairs)  95.4 us
    ppermute x1, waiting for transfers between devices, bwd_body(): lax.ppermute(dk_blk + d_key, 'cp', send_pairs)  86.9 us
    ppermute x1, waiting for transfers between devices, local_step(): d_key = lax.ppermute(carry[2] + d_key, 'cp', send_pairs)  85.1 us
    psum x1, waiting for transfers between devices, reduce_grad(): lax.psum(lax.psum_scatter(full_grad, 'fsdp', scatter_dimension=axis_dim,...  76.3 us
    psum x1, waiting for transfers between devices, local_step(): lax.psum(d_table, ('cp', 'fsdp'))  54.6 us
    convert_element_type x1, other arithmetic, local_step(): gelu_out = gelu32.astype(jnp.bfloat16)  50.5 us
  transfers between devices with their start and end apart: 16, of which 11 were waited for; matrix products, arithmetic and copies ran while one was open for 29% of the time, Pallas kernels for 0%

commit v1 on v0

v1 whole, which is shorter than its diff:
```python
import functools

import jax
import jax.numpy as jnp
from jax import lax
from jax.experimental import pallas as pl
from jax.experimental.pallas import tpu as pltpu
from jax.sharding import PartitionSpec as P

MASK_ID = 32
PAD_ID = 1
NCLS = 32
LN_EPS = 1e-5
ROPE_BASE = 10000.0
TRAIN_RATIO = 0.15 * 0.8
NEG_BIG = -1e30
BF = jnp.bfloat16
F32 = jnp.float32
VMEM_LIMIT = 60 * 1024 * 1024
NN = (((1,), (0,)), ((), ()))
NT = (((1,), (1,)), ((), ()))
TN = (((0,), (0,)), ((), ()))


def mm(a, b, dims):
    return lax.dot_general(a, b, dims, preferred_element_type=F32)


def split3(x):
    hi = x.astype(BF)
    rest = x - hi.astype(F32)
    mid = rest.astype(BF)
    lo = (rest - mid.astype(F32)).astype(BF)
    return hi, mid, lo


def one_hot_rows(cls):
    return (lax.broadcasted_iota(jnp.int32, (NCLS, cls.shape[-1]), 0) == cls).astype(BF)


def key_rows(pos, length):
    row = lax.broadcasted_iota(jnp.int32, (16, pos.shape[-1]), 0)
    bias = jnp.where(pos < length, 0.0, NEG_BIG)
    return jnp.where(row == 0, bias, jnp.where(row < 4, 1.0, 0.0)).astype(BF)


def rope_fwd(lo, hi, cos, sin):
    return jnp.concatenate([lo * cos - hi * sin, hi * cos + lo * sin], axis=0)


def attn_fwd_kernel(n_heads, hd, lens, cls_ref, pos_ref, cos_ref, sin_ref, hc_ref, w_ref, b_ref,
                    qkv_ref, o_ref, lse_ref, class_scr, lin_scr):
    step = pl.program_id(0)
    dim = n_heads * hd

    @pl.when(step == 0)
    def _():
        full = mm(hc_ref[...], w_ref[...], NN) + b_ref[...]
        class_scr[:, :dim] = full[:, :dim] * hd ** -0.5
        class_scr[:, dim:] = full[:, dim:]

    rows = class_scr[pl.ds(step * NCLS, NCLS), :]
    hot = one_hot_rows(cls_ref[0])
    hot3 = jnp.concatenate([hot, hot, hot], axis=0)
    for part in range(3):
        cols = slice(part * dim, (part + 1) * dim)
        lin_scr[cols, :] = mm(jnp.concatenate(split3(rows[:, cols]), axis=0), hot3, TN)
    length = lens[step]
    kx = key_rows(pos_ref[...], length)
    qrow = lax.broadcasted_iota(jnp.int32, kx.shape, 0)
    qx = jnp.where(qrow == 0, 1.0, 0.0).astype(BF)
    cos, sin = cos_ref[...], sin_ref[...]
    half = hd // 2

    def head(h):
        base = pl.multiple_of(h * hd, hd)
        q = rope_fwd(lin_scr[pl.ds(base, half), :], lin_scr[pl.ds(base + half, half), :], cos, sin).astype(BF)
        k = rope_fwd(lin_scr[pl.ds(dim + base, half), :], lin_scr[pl.ds(dim + base + half, half), :], cos, sin).astype(BF)
        v = lin_scr[pl.ds(2 * dim + base, hd), :].astype(BF)
        qkv_ref[0, pl.ds(base, hd), :] = q
        qkv_ref[0, pl.ds(dim + base, hd), :] = k
        qkv_ref[0, pl.ds(2 * dim + base, hd), :] = v
        s = mm(jnp.concatenate([k, kx], axis=0), jnp.concatenate([q, qx], axis=0), TN)
        top = jnp.max(s, axis=0, keepdims=True)
        p = jnp.exp(s - top)
        tot = jnp.sum(p, axis=0, keepdims=True)
        o = mm(v, p.astype(BF), NN)
        o_ref[0, pl.ds(base, hd), :] = o / tot
        lse_ref[0, pl.ds(h, 1), :] = top + jnp.log(tot)

    def body(i, carry):
        for u in range(4):
            head(i * 4 + u)
        return carry

    lax.fori_loop(0, n_heads // 4, body, 0)


def ffn_kernel(n_heads, hd, nsq, slen, ftile,
               scales, cls_ref, o_ref, gm_ref, gp_ref, et_ref, vecs_ref, bup_ref, wo_ref, wu_ref, wd_ref,
               outm_ref, outp_ref, do_ref, delta_ref, csum_ref, dvec_ref, dbup_ref, dwo_ref, dwu_ref, dwd_ref,
               x_scr, xh_scr, rs_scr, n_scr, g_scr, y_scr, dn_scr):
    step = pl.program_id(0)
    dim = n_heads * hd
    halfs = slen // 2

    @pl.when(step == 0)
    def _():
        dvec_ref[...] = jnp.zeros_like(dvec_ref)
        dbup_ref[...] = jnp.zeros_like(dbup_ref)
        dwo_ref[...] = jnp.zeros_like(dwo_ref)
        dwu_ref[...] = jnp.zeros_like(dwu_ref)
        dwd_ref[...] = jnp.zeros_like(dwd_ref)

    for i in range(nsq):
        r = slice(i * slen, (i + 1) * slen)
        hot = one_hot_rows(cls_ref[i])
        e = mm(hot, et_ref[...], TN) * scales[step * nsq + i]
        x1 = e + mm(o_ref[i].astype(BF), wo_ref[...], TN) + vecs_ref[5:6, :]
        x_scr[r, :] = x1
        mean = jnp.mean(x1, axis=-1, keepdims=True)
        cen = x1 - mean
        rstd = lax.rsqrt(jnp.mean(cen * cen, axis=-1, keepdims=True) + LN_EPS)
        xh = cen * rstd
        xh_scr[r, :] = xh
        rs_scr[r, :] = rstd
        n_scr[r, :] = (xh * vecs_ref[6:7, :] + vecs_ref[7:8, :]).astype(BF)
        g_scr[i * slen:i * slen + halfs, :] = gm_ref[i]
        g_scr[i * slen + halfs:(i + 1) * slen, :] = gp_ref[i]

    y_scr[...] = jnp.zeros_like(y_scr)
    dn_scr[...] = jnp.zeros_like(dn_scr)

    def body(j, carry):
        c = pl.ds(pl.multiple_of(j * ftile, ftile), ftile)
        n = n_scr[...]
        g = g_scr[...]
        wu = wu_ref[:, c]
        wd = wd_ref[c, :]
        u = mm(n, wu, NN) + bup_ref[:, c]
        phi = 0.5 + 0.5 * lax.erf(u * 0.7071067811865476)
        a = (u * phi).astype(BF)
        slope = phi + u * (jnp.exp(-0.5 * u * u) * 0.3989422804014327)
        y_scr[...] += mm(a, wd, NN)
        du = mm(g, wd, NT) * slope
        dub = du.astype(BF)
        dbup_ref[:, c] += jnp.sum(du, axis=0, keepdims=True)
        dwd_ref[c, :] += mm(a, g, TN)
        dwu_ref[:, c] += mm(n, dub, TN)
        dn_scr[...] += mm(dub, wu, NT)
        return carry

    lax.fori_loop(0, wu_ref.shape[1] // ftile, body, 0)

    for i in range(nsq):
        r = slice(i * slen, (i + 1) * slen)
        out = (x_scr[r, :] + y_scr[r, :] + vecs_ref[8:9, :]).astype(BF)
        outm_ref[i] = out[:halfs]
        outp_ref[i] = out[halfs:]
        dn = dn_scr[r, :]
        xh = xh_scr[r, :]
        dy = dn * vecs_ref[6:7, :]
        m1 = jnp.mean(dy, axis=-1, keepdims=True)
        m2 = jnp.mean(dy * xh, axis=-1, keepdims=True)
        g32 = g_scr[r, :].astype(F32)
        dx = g32 + rs_scr[r, :] * (dy - m1 - xh * m2)
        dvec_ref[0:1, :] += jnp.sum(dx, axis=0, keepdims=True)
        dvec_ref[1:2, :] += jnp.sum(dn * xh, axis=0, keepdims=True)
        dvec_ref[2:3, :] += jnp.sum(dn, axis=0, keepdims=True)
        dvec_ref[3:4, :] += jnp.sum(g32, axis=0, keepdims=True)
        dxb = dx.astype(BF)
        o = o_ref[i]
        dwo_ref[...] += mm(o.astype(BF), dxb, NN)
        do = mm(wo_ref[...], dxb, NT)
        do_ref[i] = do.astype(BF)
        delta_ref[i, 0:n_heads, :] = jnp.sum((do * o).reshape(n_heads, hd, slen), axis=1)
        csum_ref[i] = mm(one_hot_rows(cls_ref[i]), dxb, NN)


def attn_bwd_kernel(n_heads, hd, lens, scales, cls_ref, pos_ref, cos_ref, sin_ref, qkv_ref, do_ref, lse_ref, delta_ref,
                    csum_ref, ec_ref, vecs_ref, w_ref,
                    dw_ref, dvec_ref, dtab_ref, dlin_scr, bsum_scr, dcls_scr):
    step = pl.program_id(0)
    n_seq = pl.num_programs(0)
    dim = n_heads * hd
    half = hd // 2

    @pl.when(step == 0)
    def _():
        bsum_scr[...] = jnp.zeros_like(bsum_scr)

    kx = key_rows(pos_ref[...], lens[step])
    row = lax.broadcasted_iota(jnp.int32, kx.shape, 0)
    cos, sin = cos_ref[...], sin_ref[...]
    ones3 = jnp.where(row < 3, 1.0, 0.0).astype(BF)

    def put(base, val):
        dlin_scr[pl.ds(base, val.shape[0]), :] = val.astype(BF)
        width = val.shape[1] // 2
        bsum_scr[pl.ds(base, val.shape[0]), :] += val[:, :width] + val[:, width:]

    def unrope(val):
        lo, hi = val[:half], val[half:]
        return jnp.concatenate([lo * cos + hi * sin, hi * cos - lo * sin], axis=0)

    def head(h):
        base = pl.multiple_of(h * hd, hd)
        q = qkv_ref[0, pl.ds(base, hd), :]
        k = qkv_ref[0, pl.ds(dim + base, hd), :]
        v = qkv_ref[0, pl.ds(2 * dim + base, hd), :]
        do = do_ref[0, pl.ds(base, hd), :]
        l1, l2, l3 = [t.astype(F32) for t in split3(-lse_ref[0, pl.ds(h, 1), :])]
        qx = jnp.where(row == 0, 1.0, jnp.where(row == 1, l1, jnp.where(row == 2, l2, jnp.where(row == 3, l3, 0.0)))).astype(BF)
        d1, d2, d3 = [t.astype(F32) for t in split3(-delta_ref[0, pl.ds(h, 1), :])]
        dx = jnp.where(row == 0, d1, jnp.where(row == 1, d2, jnp.where(row == 2, d3, 0.0))).astype(BF)
        p = jnp.exp(mm(jnp.concatenate([k, kx], axis=0), jnp.concatenate([q, qx], axis=0), TN))
        dp = mm(jnp.concatenate([v, ones3], axis=0), jnp.concatenate([do, dx], axis=0), TN)
        pb = p.astype(BF)
        ds = (p * dp).astype(BF)
        dv = mm(do, pb, NT)
        dk = mm(q, ds, NT)
        dq = mm(k, ds, NN)
        put(base, unrope(dq) * hd ** -0.5)
        put(dim + base, unrope(dk))
        put(2 * dim + base, dv)

    def body(i, carry):
        for u in range(2):
            head(i * 2 + u)
        return carry

    lax.fori_loop(0, n_heads // 2, body, 0)
    hot = one_hot_rows(cls_ref[0])
    dcls_scr[pl.ds(pl.multiple_of(step * NCLS, NCLS), NCLS), :] = mm(hot, dlin_scr[...], NT)

    @pl.when(step == n_seq - 1)
    def _():
        e = ec_ref[...]
        cen = e - jnp.mean(e, axis=-1, keepdims=True)
        rstd = lax.rsqrt(jnp.mean(cen * cen, axis=-1, keepdims=True) + LN_EPS)
        xh = cen * rstd
        hc = (xh * vecs_ref[0:1, :] + vecs_ref[1:2, :]).astype(BF)
        acc = dcls_scr[...]
        hi = acc.astype(BF)
        lo = (acc - hi.astype(F32)).astype(BF)
        dw_ref[...] = mm(jnp.concatenate([hc, hc], axis=0), jnp.concatenate([hi, lo], axis=0), TN)
        dn = mm(hi, w_ref[...], NT) + mm(lo, w_ref[...], NT)
        dy = dn * vecs_ref[0:1, :]
        m1 = jnp.mean(dy, axis=-1, keepdims=True)
        m2 = jnp.mean(dy * xh, axis=-1, keepdims=True)
        de = rstd * (dy - m1 - xh * m2)
        dvec_ref[0:1, :] = jnp.sum(dn * xh, axis=0, keepdims=True)
        dvec_ref[1:2, :] = jnp.sum(dn, axis=0, keepdims=True)
        bias = jnp.sum(bsum_scr[...], axis=-1, keepdims=True)
        bias = jnp.transpose(jnp.broadcast_to(bias, (3 * dim, 128)))
        for part in range(3):
            dvec_ref[2 + part:3 + part, :] = bias[0:1, part * dim:(part + 1) * dim]
        tab = jnp.zeros((NCLS, dim), F32)
        for b in range(dcls_scr.shape[0] // NCLS):
            tab = tab + (de[b * NCLS:(b + 1) * NCLS] + csum_ref[b]) * scales[b]
        keep = lax.broadcasted_iota(jnp.int32, tab.shape, 0) != PAD_ID
        dtab_ref[...] = jnp.where(keep, tab, 0.0)


def whole(shape):
    return pl.BlockSpec(shape, lambda *_: (0,) * len(shape), pipeline_mode=pl.Buffered(1))


def params(sem="arbitrary"):
    return pltpu.CompilerParams(dimension_semantics=(sem,), vmem_limit_bytes=VMEM_LIMIT)


SMEM = pl.BlockSpec(memory_space=pltpu.SMEM)


def attn_fwd(lens, cls, pos, cos, sin, hc, w, bias, n_heads, hd):
    n_seq, _, slen = cls.shape
    dim = n_heads * hd
    return pl.pallas_call(
        functools.partial(attn_fwd_kernel, n_heads, hd),
        grid=(n_seq,),
        in_specs=[SMEM, pl.BlockSpec((1, 1, slen), lambda i: (i, 0, 0)), whole(pos.shape), whole(cos.shape),
                  whole(sin.shape), whole(hc.shape), whole(w.shape), whole(bias.shape)],
        out_specs=[pl.BlockSpec((1, 3 * dim, slen), lambda i: (i, 0, 0)), pl.BlockSpec((1, dim, slen), lambda i: (i, 0, 0)),
                   pl.BlockSpec((1, n_heads, slen), lambda i: (i, 0, 0))],
        out_shape=[jax.ShapeDtypeStruct((n_seq, 3 * dim, slen), BF), jax.ShapeDtypeStruct((n_seq, dim, slen), F32),
                   jax.ShapeDtypeStruct((n_seq, n_heads, slen), F32)],
        scratch_shapes=[pltpu.VMEM((n_seq * NCLS, 3 * dim), F32), pltpu.VMEM((3 * dim, slen), F32)],
        compiler_params=params(), name="attn_fwd",
        cost_estimate=pl.CostEstimate(flops=20 * 10**9, bytes_accessed=18 * 10**6, transcendentals=10**7),
    )(lens, cls, pos, cos, sin, hc, w, bias)


def ffn(scales, cls, o, gm, gp, etab, vecs, bup, wo, wu, wd, n_heads, hd, nsq=2, ftile=512):
    n_seq, _, slen = cls.shape
    dim, ff = wu.shape
    rows = nsq * slen
    blk = lambda *s: pl.BlockSpec((nsq,) + s, lambda i: (i,) + (0,) * len(s))
    sds = jax.ShapeDtypeStruct
    return pl.pallas_call(
        functools.partial(ffn_kernel, n_heads, hd, nsq, slen, ftile),
        grid=(n_seq // nsq,),
        in_specs=[SMEM, blk(1, slen), blk(dim, slen), blk(slen // 2, dim), blk(slen // 2, dim), whole(etab.shape),
                  whole(vecs.shape), whole(bup.shape), whole(wo.shape), whole(wu.shape), whole(wd.shape)],
        out_specs=[blk(slen // 2, dim), blk(slen // 2, dim), blk(dim, slen), blk(n_heads, slen), blk(NCLS, dim),
                   whole((4, dim)), whole((1, ff)), whole((dim, dim)), whole((dim, ff)), whole((ff, dim))],
        out_shape=[sds((n_seq, slen // 2, dim), BF), sds((n_seq, slen // 2, dim), BF), sds((n_seq, dim, slen), BF),
                   sds((n_seq, n_heads, slen), F32), sds((n_seq, NCLS, dim), F32), sds((4, dim), F32), sds((1, ff), F32),
                   sds((dim, dim), F32), sds((dim, ff), F32), sds((ff, dim), F32)],
        scratch_shapes=[pltpu.VMEM((rows, dim), F32), pltpu.VMEM((rows, dim), F32), pltpu.VMEM((rows, 1), F32),
                        pltpu.VMEM((rows, dim), BF), pltpu.VMEM((rows, dim), BF), pltpu.VMEM((rows, dim), F32),
                        pltpu.VMEM((rows, dim), F32)],
        compiler_params=params(), name="ffn",
        cost_estimate=pl.CostEstimate(flops=60 * 10**9, bytes_accessed=40 * 10**6, transcendentals=10**7),
    )(scales, cls, o, gm, gp, etab, vecs, bup, wo, wu, wd)


def attn_bwd(lens, scales, cls, pos, cos, sin, qkv, do, lse, delta, csum, ec, vecs, w, n_heads, hd):
    n_seq, _, slen = cls.shape
    dim = n_heads * hd
    blk = lambda *s: pl.BlockSpec((1,) + s, lambda i: (i,) + (0,) * len(s))
    sds = jax.ShapeDtypeStruct
    return pl.pallas_call(
        functools.partial(attn_bwd_kernel, n_heads, hd),
        grid=(n_seq,),
        in_specs=[SMEM, SMEM, blk(1, slen), whole(pos.shape), whole(cos.shape), whole(sin.shape), blk(3 * dim, slen),
                  blk(dim, slen), blk(n_heads, slen), blk(n_heads, slen), whole(csum.shape), whole(ec.shape),
                  whole(vecs.shape), whole(w.shape)],
        out_specs=[whole((dim, 3 * dim)), whole((5, dim)), whole((NCLS, dim))],
        out_shape=[sds((dim, 3 * dim), F32), sds((5, dim), F32), sds((NCLS, dim), F32)],
        scratch_shapes=[pltpu.VMEM((3 * dim, slen), BF), pltpu.VMEM((3 * dim, slen // 2), F32),
                        pltpu.VMEM((n_seq * NCLS, 3 * dim), F32)],
        compiler_params=params(), name="attn_bwd",
        cost_estimate=pl.CostEstimate(flops=40 * 10**9, bytes_accessed=20 * 10**6, transcendentals=10**7),
    )(lens, scales, cls, pos, cos, sin, qkv, do, lse, delta, csum, ec, vecs, w)


def reduce_grad(full_grad, axis_dim):
    return lax.psum(lax.psum_scatter(full_grad, 'fsdp', scatter_dimension=axis_dim, tiled=True), 'cp')


def solution(mesh):
    swap = [(0, 1), (1, 0)]

    def local_step(tokens, lengths, embed_table, layer_vecs, w_qkv, w_out, w_up, b_up, w_down, grad_out):
        cp_index = lax.axis_index('cp')
        n_all, seq_half = tokens.shape
        n_seq = n_all // 2
        slen = 2 * seq_half
        vocab, dim = embed_table.shape
        n_heads, hd = w_qkv.shape[2], w_qkv.shape[3]

        def mine(z):
            return lax.dynamic_slice_in_dim(z, cp_index * n_seq, n_seq, 0)

        def other(z):
            return lax.dynamic_slice_in_dim(z, (1 - cp_index) * n_seq, n_seq, 0)

        tok_peer = lax.ppermute(other(tokens), 'cp', swap)
        g_peer = lax.ppermute(other(grad_out), 'cp', swap)
        g_mine = mine(grad_out)
        tok = jnp.concatenate([mine(tokens), tok_peer], axis=1)
        lens = mine(lengths)
        w_qkv2 = lax.all_gather(w_qkv.reshape(w_qkv.shape[0], -1), 'fsdp', axis=0, tiled=True)
        vecs = lax.all_gather(layer_vecs, 'fsdp', axis=1, tiled=True)
        out_w = lax.all_gather(w_out, 'fsdp', axis=0, tiled=True)
        up_w = lax.all_gather(w_up, 'fsdp', axis=0, tiled=True)
        up_b = lax.all_gather(b_up, 'fsdp', axis=0, tiled=True)
        down_w = lax.all_gather(w_down, 'fsdp', axis=0, tiled=True)

        seq_pos = jnp.arange(seq_half)
        pos = jnp.concatenate([cp_index * seq_half + seq_pos, (1 - cp_index) * seq_half + seq_pos])
        inv_freq = 1.0 / (ROPE_BASE ** (jnp.arange(0, hd, 2, dtype=F32) / hd))
        angles = inv_freq[:, None] * pos.astype(F32)[None, :]
        cos_t, sin_t = jnp.cos(angles), jnp.sin(angles)
        is_mask = tok == MASK_ID
        count = jnp.sum(is_mask.astype(jnp.int32), axis=1)
        scales = (1.0 - TRAIN_RATIO) / (1.0 - count.astype(F32) / lens.astype(F32))
        cls = jnp.where(is_mask | (pos[None, :] >= lens[:, None]), PAD_ID, tok)[:, None, :]
        etab = jnp.where(jnp.arange(NCLS)[:, None] == PAD_ID, 0, embed_table[:NCLS])
        e_cls = (etab.astype(F32)[None] * scales[:, None, None]).reshape(n_seq * NCLS, dim)
        cen = e_cls - jnp.mean(e_cls, axis=-1, keepdims=True)
        var = jnp.mean(cen * cen, axis=-1, keepdims=True)
        hc = (cen * lax.rsqrt(var + LN_EPS) * vecs[0] + vecs[1]).astype(BF)
        pos2 = pos[None, :].astype(jnp.int32)

        qkv, o, lse = attn_fwd(lens, cls, pos2, cos_t, sin_t, hc, w_qkv2, vecs[2:5].reshape(1, 3 * dim), n_heads, hd)
        (out_m, out_p, do, delta, csum, dvec_b, d_bup, d_wo, d_wu, d_wd) = ffn(
            scales, cls, o, g_mine, g_peer, etab, vecs, up_b[None, :], out_w, up_w, down_w, n_heads, hd)
        out_back = lax.ppermute(out_p, 'cp', swap)
        layer_out = jnp.where(cp_index == 0, jnp.concatenate([out_m, out_back], 0), jnp.concatenate([out_back, out_m], 0))
        d_w, dvec_a, d_tab = attn_bwd(lens, scales, cls, pos2, cos_t, sin_t, qkv, do, lse, delta, csum, e_cls, vecs, w_qkv2,
                                      n_heads, hd)
        d_table = jnp.concatenate([d_tab, jnp.zeros((vocab - NCLS, dim), F32)], 0)
        d_vecs = jnp.concatenate([dvec_a, dvec_b], 0)
        return (layer_out, lax.psum(d_table, ('cp', 'fsdp')), reduce_grad(d_vecs, 1),
                reduce_grad(d_w, 0).reshape(w_qkv.shape), reduce_grad(d_wo, 0), reduce_grad(d_wu, 0),
                reduce_grad(d_bup[0], 0), reduce_grad(d_wd, 0))

    in_specs = (P('fsdp', 'cp'), P('fsdp'), P(), P(None, 'fsdp'), P('fsdp', None, None, None), P('fsdp', None), P('fsdp', None), P('fsdp'), P('fsdp', None), P('fsdp', 'cp', None))
    out_specs = (P('fsdp', 'cp', None), P(), P(None, 'fsdp'), P('fsdp', None, None, None), P('fsdp', None), P('fsdp', None), P('fsdp'), P('fsdp', None))
    return jax.shard_map(local_step, mesh=mesh, in_specs=in_specs, out_specs=out_specs, check_vma=False)
```

time: 1270 us -> 667 us (0.53)
  waiting for transfers between devices: 671 us -> 344 us
  matrix products: 323 us -> 0 us
  Pallas kernels: 0 us -> 197 us
  other arithmetic: 111 us -> 5.71 us
  local copies, waits for them, and re-layouts: 53 us -> 21.6 us
    ppermute x6 -> x3, waiting for transfers between devices: 382 us -> 0.01 us  [the longest x1 0.01 us: local_step(): g_peer = lax.ppermute(other(grad_out), 'cp', swap)]
    dot_general x26 -> x0, matrix products: 323 us -> none  [the longest x1 34.4 us: local_step(): jnp.einsum('bsthe,dthe->bsd', d_qkv_b, qkv_w, preferred_element_type=jnp....]
    pallas_call x0 -> x3, Pallas kernels: none -> 197 us  [the longest x1 76.3 us: ffn(): pl.pallas_call(functools.partial(ffn_kernel, n_heads, hd, nsq, slen, ftil...]
    reduce_scatter x3 -> x4, waiting for transfers between devices: 114 us -> 199 us  [reduce_grad(): lax.psum_scatter(full_grad, 'fsdp', scatter_dimension=axis_dim, tiled=True)]
    convert_element_type x3 -> x2, other arithmetic: 51.1 us -> 0.71 us  [the longest x1 0.7 us: local_step(): etab.astype(F32)[None] * scales[:, None, None]]
    all_gather x1, waiting for transfers between devices: 42.2 us -> 0.01 us  [local_step(): lax.all_gather(w_qkv.reshape(w_qkv.shape[0], -1), 'fsdp', axis=0, tiled=T...]
    reduce_sum x9 -> x3, other arithmetic: 37.2 us -> 0.53 us  [the longest x1 0.23 us: local_step(): var = jnp.mean(cen * cen, axis=-1, keepdims=True)]
    unnamed x141 -> x50, local copies, waits for them, and re-layouts: 34.2 us -> 11.9 us
  transfers between devices with their start and end apart: 16 -> 13, of which waited for: 11 -> 7; matrix products, arithmetic and copies ran while one was open for 29% -> 3% of each run, Pallas kernels for 0% -> 9%
where the time goes in v1:
time: 667 us
  waiting for transfers between devices  344 us (52%)
  Pallas kernels  197 us (30%)
  blocking collectives  76.8 us (12%)
  local copies, waits for them, and re-layouts  21.6 us (3%)
  between operations  15.7 us (2%)
    reduce_scatter x4, waiting for transfers between devices, reduce_grad(): lax.psum_scatter(full_grad, 'fsdp', scatter_dimension=axis_dim, tiled=True)  199 us
    psum x1, waiting for transfers between devices, reduce_grad(): lax.psum(lax.psum_scatter(full_grad, 'fsdp', scatter_dimension=axis_dim,...  76.3 us
    pallas_call x1, Pallas kernels, ffn(): pl.pallas_call(functools.partial(ffn_kernel, n_heads, hd, nsq, slen, ftil...  76.3 us
    pallas_call x1, Pallas kernels, attn_bwd(): pl.pallas_call(functools.partial(attn_bwd_kernel, n_heads, hd), grid=(n_s...  64.2 us
    psum x1, waiting for transfers between devices, local_step(): lax.psum(d_table, ('cp', 'fsdp'))  58.6 us
    pallas_call x1, Pallas kernels, attn_fwd(): pl.pallas_call(functools.partial(attn_fwd_kernel, n_heads, hd), grid=(n_s...  56.9 us
    unnamed x2, blocking collectives  46.3 us
  transfers between devices with their start and end apart: 13, of which 7 were waited for; matrix products, arithmetic and copies ran while one was open for 3% of the time, Pallas kernels for 9%

profile of v1, /device:TPU:0, one launch (start us, length us, event | category | flops | bytes accessed | tf_op | source)
XLA Modules:
  0.0 666.8 jit_solution(14109287657428728261)
XLA Ops:
  7.2 1.9 copy.25
  9.2 0.7 all-gather.7.cloned.1.call-update
  10.0 0.7 all-gather.9.cloned.1.call-update
  10.7 0.7 constant_dynamic-slice_fusion.3
  11.5 3.3 collective-permute-start
  14.8 3.1 constant_dynamic-slice_fusion
  18.0 9.7 %all-gather = f32[8,80,9]{1,2,0:T(8,128)S(1)} all-gather(f32[1,80,9]{1,2,0:T(8,128)S(1)} %bitcast.33), channel_id=1, replica_groups=mesh['cp'=2,'fsdp'=8] {'fsdp'}, dimensions={0}, use_global_device_ids=true | all-gather | bytes 25920 | tf_op jit(solution)/shard_map/all_gather | solution.py:365
  27.8 0.7 fusion.4
  29.1 0.3 dynamic-update-slice
  29.5 12.2 %all_gather.21.wo_ref = bf16[640,640]{1,0:T(8,128)(2,1)} all-gather(bf16[80,640]{1,0:T(8,128)(2,1)S(1)} %copy-done.3), channel_id=1, replica_groups=mesh['cp'=2,'fsdp'=8] {'fsdp'}, dimensions={0}, use_global_device_ids=true | all-gather | bytes 921600 | tf_op jit(solution)/shard_map/all_gather | solution.py:366
  41.7 0.8 multiply_sine_fusion
  42.4 0.7 fusion.3
  43.1 23.8 %all-reduce.1 = f32[2560]{0:T(1024)S(1)} all-reduce(f32[2560]{0:T(1024)S(1)} %dynamic-update-slice), channel_id=1, replica_groups=mesh['cp'=2,'fsdp'=8] {'fsdp'}, use_global_device_ids=true, to_apply=%add.1 | all-reduce | flops 2560 | bytes 20480
  66.9 0.6 broadcast_in_dim.37.bup_ref
  67.5 0.6 copy.29
  68.1 0.1 convert_reduce_fusion
  68.2 0.1 subtract_divide_fusion
  68.5 0.2 multiply_reduce_fusion
  68.8 0.2 fusion.1
  69.1 1.1 bitcast_multiply_fusion
  70.2 0.7 or_select_fusion.cls_ref
  70.9 56.9 %attn_fwd.1 = (bf16[8,1920,256]{2,1,0:T(8,128)(2,1)}, f32[8,640,256]{2,1,0:T(8,128)}, f32[8,20,256]{2,1,0:T(8,128)}) custom-call(s32[8]{0:T(128)} %copy-done.14, s32[8,1,256]{2,1,0:T(1,128)} %or_select_fusion.cls_ref, s32[1,256]{1,0:T(1,128)} %bitcast.35, f32[16,256]{1,0:T(8,128)} %get-tuple-element.59.cos_ref, f32[16,256]{1,0:T(8,128)} %get-tuple-element.58.sin_ref, ...), custom_call_target="tpu_custom_call" | custom-call | flops 20000000000 | bytes 18000000 | tf_op jit(solution)/shard_map/attn_fwd/pallas_call | solution.py:279
  127.9 1.1 copy-done.17
  129.0 76.3 %ffn.1 = (bf16[8,128,640]{2,1,0:T(8,128)(2,1)}, bf16[8,128,640]{2,1,0:T(8,128)(2,1)}, bf16[8,640,256]{2,1,0:T(8,128)(2,1)}, f32[8,20,256]{2,1,0:T(8,128)}, f32[8...) custom-call(f32[8]{0:T(128)} %copy-done.10, ...), custom_call_target="tpu_custom_call" | custom-call | flops 60000002048 | bytes 40000000 | tf_op jit(solution)/shard_map/ffn/pallas_call | solution.py:300
  205.3 64.2 %attn_bwd.1 = (f32[640,1920]{1,0:T(8,128)}, f32[5,640]{1,0:T(8,128)}, f32[32,640]{1,0:T(8,128)}) custom-call(s32[8]{0:T(128)} %copy-done.14, f32[8]{0:T(128)} %copy-done.10, s32[8,1,256]{2,1,0:T(1,128)} %or_select_fusion.cls_ref, s32[1,256]{1,0:T(1,128)} %bitcast.36, f32[16,256]{1,0:T(8,128)} %get-tuple-element.59.cos_ref, ...), custom_call_target="tpu_custom_call" | custom-call | flops 40000000000 | bytes 20000000 | tf_op jit(solution)/shard_map/attn_bwd/pallas_call | solution.py:323
  269.6 0.5 reduce-scatter.10.cloned.1.call-update
  270.2 0.5 reduce-scatter.12.cloned.1.call-update
  270.8 0.7 reduce-scatter.14.cloned.1.call-update
  271.6 0.9 copy.27
  272.6 0.7 concatenate.48
  273.3 45.1 %reduce-scatter.8.cloned.1.call-done = f32[80,1920]{1,0:T(8,128)} async-done(((f32[640,1920]{1,0:T(8,128)}), f32[80,1920]{1,0:T(8,128)}) %reduce-scatter.8.cloned.1.call-update) | async-done | bytes 614416 | tf_op jit(solution)/shard_map/reduce_scatter | solution.py:339
  318.4 2.4 copy.26
  320.7 33.7 %reduce-scatter.10.cloned.1.call-done = f32[80,640]{1,0:T(8,128)} async-done(((f32[640,640]{1,0:T(8,128)}), f32[80,640]{1,0:T(8,128)}) %reduce-scatter.10.cloned.1.call-update) | async-done | bytes 204816 | tf_op jit(solution)/shard_map/reduce_scatter | solution.py:339
  354.4 60.0 %reduce-scatter.12.cloned.1.call-done = f32[80,2560]{1,0:T(8,128)} async-done(((f32[640,2560]{1,0:T(8,128)}), f32[80,2560]{1,0:T(8,128)}) %reduce-scatter.12.cloned.1.call-update) | async-done | bytes 819216 | tf_op jit(solution)/shard_map/reduce_scatter | solution.py:339
  414.4 60.2 %reduce-scatter.14.cloned.1.call-done = f32[320,640]{1,0:T(8,128)} async-done(((f32[2560,640]{1,0:T(8,128)}), f32[320,640]{1,0:T(8,128)}) %reduce-scatter.14.cloned.1.call-update) | async-done | bytes 819216 | tf_op jit(solution)/shard_map/reduce_scatter | solution.py:339
  474.6 1.5 collective-permute-start.2
  476.8 22.5 %all-reduce.2 = f32[2560]{0:T(1024)S(1)} all-reduce(f32[2560]{0:T(1024)S(1)} %reduce.4), channel_id=6, replica_groups=mesh['cp'=2,'fsdp'=8] {'fsdp'}, use_global_device_ids=true, to_apply=%region_12.13.clone | all-reduce | flops 2560 | bytes 20480
  499.4 7.0 %reduce-scatter.16.cloned.1.call-done = f32[80,9]{1,0:T(8,128)} async-done(((f32[640,9]{1,0:T(8,128)}), f32[80,9]{1,0:T(8,128)}) %reduce-scatter.16.cloned.1.call-update) | async-done | bytes 2896
  506.4 0.8 copy.28
  507.3 8.6 %all-reduce.3 = (f32[9,80]{1,0:T(8,128)}, f32[320]{0:T(512)}) all-reduce(f32[9,80]{1,0:T(8,128)S(1)} %copy.28, f32[320]{0:T(512)S(1)} %dynamic-slice.2), channel_id=1, replica_groups=mesh['cp'=2,'fsdp'=8] {'cp'}, use_global_device_ids=true, to_apply=%region_5.6 | all-reduce | flops 1040 | bytes 8320 | tf_op jit(solution)/shard_map/psum | solution.py:339
  515.9 1.8 maximum_select_fusion
  517.7 58.6 %all-reduce.8.cloned.1.call-done = f32[33,640]{1,0:T(8,128)} async-done(((f32[33,640]{1,0:T(8,128)}), f32[33,640]{1,0:T(8,128)}) %all-reduce.8.cloned.1.call-update) | async-done | bytes 84496 | tf_op jit(solution)/shard_map/psum | solution.py:396
  576.3 76.3 %all-reduce.10.cloned.1.call-done = (f32[80,3,20,32]{0,3,2,1:T(8,128)}, f32[80,640]{1,0:T(8,128)}, f32[80,2560]{1,0:T(8,128)}, f32[320,640]{1,0:T(8,128)}) async-done(((f32[80,3,20,32]{0,3,2,1:T(8,128)}, f32[80,640]{1,0:T(8,128)}, f32[80,2560]{1,0:T(8,128)}, f32[320,640]{1,0:T(8,128)}), (f32[80,3,20,32]{0,3,2,1:T(8,128)}, f32[80,640]{1,0:T(8,128)}, f32[80,2560]{1,0:T(8,128)}, ...) | async-done | bytes 2457616 | tf_op jit(solution)/shard_map/psum | solution.py:339
  652.6 1.7 copy.36
  654.3 2.2 copy.37
  656.5 1.6 copy.38
  658.1 0.9 copy.39
  659.0 0.9 copy.40
  (75 shorter events, 1.3 us)
Async XLA Ops:
  7.2 63.7 %all-gather.5.cloned.1.call-start = ((), (), s32[]{:S(2)}) async-start(), calls=%async_computation.5 | async-start | bytes 2764800 | tf_op jit(solution)/shard_map/all_gather | solution.py:364
  9.2 118.7 %all-gather.7.cloned.1.call-start = ((), (), s32[]{:S(2)}) async-start(), calls=%async_computation.6 | async-start | bytes 3686400 | tf_op jit(solution)/shard_map/all_gather | solution.py:367
  9.9 118.0 %all-gather.9.cloned.1.call-start = ((), (), s32[]{:S(2)}) async-start(), calls=%async_computation.7 | async-start | bytes 3686400 | tf_op jit(solution)/shard_map/all_gather | solution.py:369
  10.7 307.7 %reduce-scatter.8.cloned.1.call-start = ((), (), s32[]{:S(2)}) async-start(), calls=%async_computation.9 | async-start | bytes 5529600 | tf_op jit(solution)/shard_map/reduce_scatter | solution.py:339
  11.4 6.5 copy-start.11
  11.4 16.3 %copy-start.13 = (u32[16]{0:T(128)S(1)}, u32[16]{0:T(128)}, u32[]{:S(2)}) copy-start(u32[16]{0:T(128)} %constant.46) | copy-start | bytes 196
  11.4 17.7 %copy-start.15 = (f32[320]{0:T(512)S(1)}, f32[320]{0:T(512)}, u32[]{:S(2)}) copy-start(f32[320]{0:T(512)} %param.17) | copy-start | bytes 3844
  11.4 18.0 %copy-start.3 = (bf16[80,640]{1,0:T(8,128)(2,1)S(1)}, bf16[80,640]{1,0:T(8,128)(2,1)}, u32[]{:S(2)}) copy-start(bf16[80,640]{1,0:T(8,128)(2,1)} %param.15) | copy-start | bytes 307204
  11.4 31.0 %copy-start.6 = (bf16[33,640]{1,0:T(8,128)(2,1)S(1)}, bf16[33,640]{1,0:T(8,128)(2,1)}, u32[]{:S(2)}) copy-start(bf16[33,640]{1,0:T(8,128)(2,1)} %param.12) | copy-start | bytes 126724
  11.5 56.8 %copy-start.16 = (s32[16]{0:T(128)S(1)}, s32[16]{0:T(128)}, u32[]{:S(2)}) copy-start(s32[16]{0:T(128)} %param.11) | copy-start | bytes 196
  11.5 56.6 %collective-permute-start = (s32[8,128]{1,0:T(8,128)S(1)}, s32[8,128]{1,0:T(8,128)S(1)}, u32[]{:S(2)}, u32[]{:S(2)}) collective-permute-start(s32[8,128]{1,0:T(8,128)S(1)} %get-tuple-element.57), channel_id=1, source_target_pairs={{0,8},{8,0},{1,9},{9,1},{2,10},{10,2},{3,11},{11,3},{4,12},{12,4},... | collective-permute-start | bytes 12296 | tf_op jit(solution)/shard_map/ppermute | solution.py:359
  17.9 109.9 %collective-permute-start.1 = (bf16[8,128,640]{2,1,0:T(8,128)(2,1)S(1)}, bf16[8,128,640]{2,1,0:T(8,128)(2,1)S(1)}, u32[]{:S(2)}, u32[]{:S(2)}) collective-permute-start(bf16[8,128,640]{2,1,0:T(8,128)(2,1)S(1)} %get-tuple-element.52), channel_id=1, source_target_pairs={{0,8},{8,0},{1,9},{9,1},{2,10},{10,2},{3,11},{11,3},{4,12},{12,4},... | collective-permute-start | bytes 3932168 | tf_op jit(solution)/shard_map/ppermute | solution.py:360
  27.8 100.1 %copy-start.5 = (f32[640,9]{0,1:T(8,128)}, f32[640,9]{0,1:T(8,128)S(1)}, u32[]{:S(2)}) copy-start(f32[640,9]{0,1:T(8,128)S(1)} %reshape.201) | copy-start | bytes 69124
  29.4 41.5 %copy-start.12 = (s32[256]{0:T(256)}, s32[256]{0:T(256)S(1)}, u32[]{:S(2)}) copy-start(s32[256]{0:T(256)S(1)} %get-tuple-element.61) | copy-start | bytes 3076
  68.3 2.6 copy-start.14
  68.3 59.5 %copy-start.10 = (f32[8]{0:T(128)}, f32[8]{0:T(128)S(1)}, u32[]{:S(2)}) copy-start(f32[8]{0:T(128)S(1)} %get-tuple-element.50.scales) | copy-start | bytes 100
  127.9 1.1 copy-start.17
  269.6 84.9 %reduce-scatter.10.cloned.1.call-start = ((), (), s32[]{:S(2)}) async-start(), calls=%async_computation.10 | async-start | bytes 1843200 | tf_op jit(solution)/shard_map/reduce_scatter | solution.py:339
  270.2 144.3 %reduce-scatter.12.cloned.1.call-start = ((), (), s32[]{:S(2)}) async-start(), calls=%async_computation.11 | async-start | bytes 7372800 | tf_op jit(solution)/shard_map/reduce_scatter | solution.py:339
  270.7 203.9 %reduce-scatter.14.cloned.1.call-start = ((), (), s32[]{:S(2)}) async-start(), calls=%async_computation.12 | async-start | bytes 7372800 | tf_op jit(solution)/shard_map/reduce_scatter | solution.py:339
  270.8 0.8 copy-start.7
  270.8 0.8 copy-start.8
  270.8 1.8 copy-start.4
  271.5 234.9 %reduce-scatter.16.cloned.1.call-start = ((), (), s32[]{:S(2)}) async-start(), calls=%async_computation.13 | async-start | bytes 368640
  272.5 204.3 %copy-start.9 = (f32[1,2560]{1,0:T(1,128)S(1)}, f32[1,2560]{1,0:T(1,128)}, u32[]{:S(2)}) copy-start(f32[1,2560]{1,0:T(1,128)} %get-tuple-element.38) | copy-start | bytes 30724
  272.5 243.4 %copy-start = (bf16[8,128,640]{2,1,0:T(8,128)(2,1)S(1)}, bf16[8,128,640]{2,1,0:T(8,128)(2,1)}, u32[]{:S(2)}) copy-start(bf16[8,128,640]{2,1,0:T(8,128)(2,1)} %get-tuple-element.25) | copy-start | bytes 3932164
  272.5 303.8 %all-reduce.8.cloned.1.call-start = ((), (), s32[]{:S(2)}) async-start(), calls=%async_computation.8 | async-start | bytes 204800 | tf_op jit(solution)/shard_map/psum | solution.py:396
  273.2 379.4 %all-reduce.10.cloned.1.call-start = ((), (), s32[]{:S(2)}) async-start(), calls=%async_computation.14 | async-start | bytes 5652480 | tf_op jit(solution)/shard_map/psum | solution.py:339
  474.6 41.3 %collective-permute-start.2 = (bf16[8,128,640]{2,1,0:T(8,128)(2,1)}, bf16[8,128,640]{2,1,0:T(8,128)(2,1)S(1)}, u32[]{:S(2)}, u32[]{:S(2)}) collective-permute-start(bf16[8,128,640]{2,1,0:T(8,128)(2,1)} %get-tuple-element.26), channel_id=1, source_target_pairs={{0,8},{8,0},{1,9},{9,1},{2,10},{10,2},{3,11},{11,3},{4,12},{12,4},... | collective-permute-start | bytes 3932168 | tf_op jit(solution)/shard_map/ppermute | solution.py:390
  652.6 5.5 copy-start.2
  652.6 6.4 copy-start.1
Sparse Core Ops, SparseCore 0:
  10.4 29.7 all-gather.4
  42.1 29.4 all-gather.6
  73.4 28.9 all-gather.8
  269.7 48.6 reduce-scatter.7
  321.5 32.8 reduce-scatter.9
  357.7 56.6 reduce-scatter.11
  417.8 56.6 reduce-scatter.13
  478.2 28.1 reduce-scatter.15
  511.2 65.0 all-reduce.7
  579.3 73.3 all-reduce.9
